TPU v7x, 32 devices: a whole 2x2x4 slice. The times are simulated.
32 devices in a mesh: row: 4 (over y, core), col: 8 (over z, x).
Axes of the slice: x: 2, y: 2, z: 4, core: 2. Of those that a mesh axis runs over, the one named last changes fastest.
Arguments:
- tile_values: bfloat16 [4, 8, 96, 256, 256], P('row', 'col')
- tile_index: int32 [4, 8, 96, 2], P('row', 'col'), may hold values from 0 to 15, as said below
- tile_count: int32 [4, 8], P('row', 'col'), may hold values from 12 to 96, as said below
- start_vectors: float32 [64, 16, 256], P(('row', 'col')), may hold values from -6 to 6
Outputs:
- iterate: float32 [64, 16, 256], P(('row', 'col'))
Inputs may be any that keep to these rules, and one draw needn't show every extreme that they name: `tile_index`: on device (r, c), slot t holds a local block row in 0 .. 15 and a local block column in 0 .. 7; the pairs of the slots below tile_count[r, c] are distinct; slots at or beyond the count are to be ignored. `tile_count`: some device uses all 96 slots.
All inputs are finite; a program needn't handle non-finite values.
Results may differ from a plain program's by a relative error of at most 0.0075.
Values may be sent and summed in bfloat16 or wider, within the bound.
A program may use at most 64 MiB of HBM per device.

v0:
```python
import jax
import jax.numpy as jnp
from jax import lax
from jax.sharding import PartitionSpec as P

ITERS = 5


epsilon = 1e-06


def column_rms(current, positions):
    local_squares = jnp.sum(current * current, axis=(0, 2))
    squares = lax.psum(local_squares, ("row", "col"))
    return jnp.sqrt(squares / positions + epsilon)


def shards(tile_values, tile_index, tile_count, start_vectors):
    stored = tile_values[0, 0]
    layout = tile_index[0, 0]
    used_count = tile_count[0, 0]
    capacity = stored.shape[0]
    own_blocks = start_vectors.shape[0]
    vector_count = start_vectors.shape[1]
    tile_size = start_vectors.shape[2]
    rows_here = lax.axis_size("col") * own_blocks
    positions = lax.axis_size("row") * lax.axis_size("col") * own_blocks * tile_size
    slot_ids = jnp.arange(capacity, dtype=jnp.int32)
    in_use = slot_ids < used_count
    local_row = layout[:, 0]
    local_col = layout[:, 1]
    block_rows = jnp.arange(rows_here, dtype=jnp.int32)
    onehot = ((block_rows[:, None] == local_row[None, :]) & in_use[None, :]).astype(jnp.float32)
    current = start_vectors
    for iteration in range(ITERS):
        rounded = current.astype(jnp.bfloat16)
        divisor = column_rms(current, positions)
        column_set = lax.all_gather(rounded, "row", axis=0, tiled=True)
        picked = jnp.take(column_set, local_col, axis=0)
        products = jnp.einsum("tkb,tab->tka", picked, stored, preferred_element_type=jnp.float32)
        flat_products = products.reshape(capacity, vector_count * tile_size)
        term = jnp.dot(onehot, flat_products, precision=lax.Precision.HIGHEST)
        summed = lax.psum_scatter(
            term.reshape(own_blocks * lax.axis_size("col"), vector_count, tile_size),
            "col",
            scatter_dimension=0,
            tiled=True,
        )
        current = summed / divisor[None, :, None]
    return current


def solution(mesh):
    return jax.shard_map(
        shards,
        mesh=mesh,
        in_specs=(
            P("row", "col", None, None, None),
            P("row", "col", None, None),
            P("row", "col"),
            P(("row", "col"), None, None),
        ),
        out_specs=P(("row", "col"), None, None),
        check_vma=False,
    )
```

profile of v0, /device:TPU:0, one launch (start us, length us, event | category | flops | bytes accessed | tf_op | source)
XLA Modules:
  0.0 414.7 jit_solution(15455334543371084319)
XLA Ops:
  6.5 0.7 slice_bitcast_fusion
  7.2 0.7 compare_and_fusion
  8.6 1.0 multiply_reduce_fusion.4
  9.5 6.2 %all_gather.15 = bf16[8,16,256]{2,1,0:T(8,128)(2,1)S(1)} all-gather(bf16[2,16,256]{2,1,0:T(8,128)(2,1)S(1)} %get-tuple-element.17), channel_id=1, replica_groups=mesh['row'=4,'col'=8] {'row'}, dimensions={0}, use_global_device_ids=true | all-gather | bytes 81920 | tf_op jit(solution)/shard_map/all_gather | solution.py:38
  15.7 0.6 gather_fusion
  16.4 8.0 %fusion.8 = f32[96,16,256]{2,1,0:T(8,128)S(1)} fusion(bf16[1,1,96,256,256]{4,3,2,1,0:T(8,128)(2,1)} %param.6, bf16[96,16,256]{2,1,0:T(8,128)(2,1)S(1)} %gather_fusion, pred[96]{0:T(512)(128)(4,1)S(1)} %get-tuple-element.6), kind=kOutput, calls=%fused_computation.13 | convolution fusion | flops 201719808 | bytes 14942304 | tf_op jit(solution)/shard_map/tkb,tab->tka/dot_general | solution.py:40
  24.3 1.5 fusion.22
  25.8 0.8 copy.21
  26.7 0.0 reduce-scatter.6.cloned.1.call-update
  26.7 0.0 reduce-scatter.8.cloned.1.call-start
  26.8 41.1 %psum.35 = f32[16]{0:T(128)S(1)} all-reduce(f32[16]{0:T(128)S(1)} %get-tuple-element.16), channel_id=1, replica_groups=mesh['row'=4,'col'=8] {'row','col'}, use_global_device_ids=true, to_apply=%region_2.0 | all-reduce | flops 16 | bytes 128 | tf_op jit(solution)/shard_map/psum | solution.py:14
  67.9 23.3 %reduce-scatter.6.cloned.1.call-done = f32[2,16,256]{2,1,0:T(8,128)} async-done(((f32[16,16,256]{2,1,0:T(8,128)}), f32[2,16,256]{2,1,0:T(8,128)}) %reduce-scatter.6.cloned.1.call-update) | async-done | bytes 32784 | tf_op jit(solution)/shard_map/reduce_scatter | solution.py:43
  91.1 0.9 multiply_reduce_fusion.3
  92.1 5.2 %all_gather.16 = bf16[8,16,256]{2,1,0:T(8,128)(2,1)S(1)} all-gather(bf16[2,16,256]{2,1,0:T(8,128)(2,1)S(1)} %get-tuple-element.15), channel_id=1, replica_groups=mesh['row'=4,'col'=8] {'row'}, dimensions={0}, use_global_device_ids=true | all-gather | bytes 81920 | tf_op jit(solution)/shard_map/all_gather | solution.py:38
  97.3 0.6 gather_fusion.1
  97.9 8.0 %fusion.6 = f32[96,16,256]{2,1,0:T(8,128)S(1)} fusion(bf16[1,1,96,256,256]{4,3,2,1,0:T(8,128)(2,1)} %param.6, bf16[96,16,256]{2,1,0:T(8,128)(2,1)S(1)} %gather_fusion.1, pred[96]{0:T(512)(128)(4,1)S(1)} %get-tuple-element.6), kind=kOutput, calls=%fused_computation.11 | convolution fusion | flops 201719808 | bytes 14942304 | tf_op jit(solution)/shard_map/tkb,tab->tka/dot_general | solution.py:40
  105.9 1.5 fusion.19
  107.4 0.8 copy.23
  108.3 0.0 reduce-scatter.10.cloned.1.call-start
  108.3 40.1 %psum.36 = f32[16]{0:T(128)S(1)} all-reduce(f32[16]{0:T(128)S(1)} %get-tuple-element.14), channel_id=1, replica_groups=mesh['row'=4,'col'=8] {'row','col'}, use_global_device_ids=true, to_apply=%region_5.7 | all-reduce | flops 16 | bytes 128 | tf_op jit(solution)/shard_map/psum | solution.py:14
  148.5 21.5 %reduce-scatter.8.cloned.1.call-done = f32[2,16,256]{2,1,0:T(8,128)} async-done(((f32[16,16,256]{2,1,0:T(8,128)}), f32[2,16,256]{2,1,0:T(8,128)}) %reduce-scatter.8.cloned.1.call-update) | async-done | bytes 32784 | tf_op jit(solution)/shard_map/reduce_scatter | solution.py:43
  169.9 0.9 multiply_reduce_fusion.2
  170.9 5.4 %all_gather.17 = bf16[8,16,256]{2,1,0:T(8,128)(2,1)S(1)} all-gather(bf16[2,16,256]{2,1,0:T(8,128)(2,1)S(1)} %get-tuple-element.13), channel_id=1, replica_groups=mesh['row'=4,'col'=8] {'row'}, dimensions={0}, use_global_device_ids=true | all-gather | bytes 81920 | tf_op jit(solution)/shard_map/all_gather | solution.py:38
  176.3 0.6 gather_fusion.2
  176.9 8.0 %fusion.4 = f32[96,16,256]{2,1,0:T(8,128)S(1)} fusion(bf16[1,1,96,256,256]{4,3,2,1,0:T(8,128)(2,1)} %param.6, bf16[96,16,256]{2,1,0:T(8,128)(2,1)S(1)} %gather_fusion.2, pred[96]{0:T(512)(128)(4,1)S(1)} %get-tuple-element.6), kind=kOutput, calls=%fused_computation.9 | convolution fusion | flops 201719808 | bytes 14942304 | tf_op jit(solution)/shard_map/tkb,tab->tka/dot_general | solution.py:40
  184.9 1.5 fusion.16
  186.4 0.8 copy.25
  187.3 0.0 reduce-scatter.12.cloned.1.call-start
  187.3 40.2 %psum.37 = f32[16]{0:T(128)S(1)} all-reduce(f32[16]{0:T(128)S(1)} %get-tuple-element.12), channel_id=1, replica_groups=mesh['row'=4,'col'=8] {'row','col'}, use_global_device_ids=true, to_apply=%region_8.10 | all-reduce | flops 16 | bytes 128 | tf_op jit(solution)/shard_map/psum | solution.py:14
  227.5 21.4 %reduce-scatter.10.cloned.1.call-done = f32[2,16,256]{2,1,0:T(8,128)} async-done(((f32[16,16,256]{2,1,0:T(8,128)}), f32[2,16,256]{2,1,0:T(8,128)}) %reduce-scatter.10.cloned.1.call-update) | async-done | bytes 32784 | tf_op jit(solution)/shard_map/reduce_scatter | solution.py:43
  248.9 0.9 multiply_reduce_fusion.1
  249.9 5.2 %all_gather.18 = bf16[8,16,256]{2,1,0:T(8,128)(2,1)S(1)} all-gather(bf16[2,16,256]{2,1,0:T(8,128)(2,1)S(1)} %get-tuple-element.11), channel_id=1, replica_groups=mesh['row'=4,'col'=8] {'row'}, dimensions={0}, use_global_device_ids=true | all-gather | bytes 81920 | tf_op jit(solution)/shard_map/all_gather | solution.py:38
  255.1 0.6 gather_fusion.3
  255.7 8.0 %fusion.2 = f32[96,16,256]{2,1,0:T(8,128)S(1)} fusion(bf16[1,1,96,256,256]{4,3,2,1,0:T(8,128)(2,1)} %param.6, bf16[96,16,256]{2,1,0:T(8,128)(2,1)S(1)} %gather_fusion.3, pred[96]{0:T(512)(128)(4,1)S(1)} %get-tuple-element.6), kind=kOutput, calls=%fused_computation.7 | convolution fusion | flops 201719808 | bytes 14942304 | tf_op jit(solution)/shard_map/tkb,tab->tka/dot_general | solution.py:40
  263.7 1.5 fusion.13
  265.2 0.8 copy.27
  266.1 0.0 reduce-scatter.14.cloned.1.call-start
  266.1 40.1 %psum.38 = f32[16]{0:T(128)S(1)} all-reduce(f32[16]{0:T(128)S(1)} %get-tuple-element.10), channel_id=1, replica_groups=mesh['row'=4,'col'=8] {'row','col'}, use_global_device_ids=true, to_apply=%region_11.13 | all-reduce | flops 16 | bytes 128 | tf_op jit(solution)/shard_map/psum | solution.py:14
  306.2 21.5 %reduce-scatter.12.cloned.1.call-done = f32[2,16,256]{2,1,0:T(8,128)} async-done(((f32[16,16,256]{2,1,0:T(8,128)}), f32[2,16,256]{2,1,0:T(8,128)}) %reduce-scatter.12.cloned.1.call-update) | async-done | bytes 32784 | tf_op jit(solution)/shard_map/reduce_scatter | solution.py:43
  327.7 0.9 multiply_reduce_fusion
  328.6 5.5 %all_gather.19 = bf16[8,16,256]{2,1,0:T(8,128)(2,1)S(1)} all-gather(bf16[2,16,256]{2,1,0:T(8,128)(2,1)S(1)} %get-tuple-element.9), channel_id=1, replica_groups=mesh['row'=4,'col'=8] {'row'}, dimensions={0}, use_global_device_ids=true | all-gather | bytes 81920 | tf_op jit(solution)/shard_map/all_gather | solution.py:38
  334.1 0.6 gather_fusion.4
  334.7 8.0 %fusion = f32[96,16,256]{2,1,0:T(8,128)S(1)} fusion(bf16[1,1,96,256,256]{4,3,2,1,0:T(8,128)(2,1)} %param.6, bf16[96,16,256]{2,1,0:T(8,128)(2,1)S(1)} %gather_fusion.4, pred[96]{0:T(512)(128)(4,1)S(1)} %get-tuple-element.6), kind=kOutput, calls=%fused_computation.5 | convolution fusion | flops 201719808 | bytes 14942304 | tf_op jit(solution)/shard_map/tkb,tab->tka/dot_general | solution.py:40
  342.7 1.5 fusion.10
  344.2 0.8 copy.29
  345.1 40.2 %psum.39 = f32[16]{0:T(128)S(1)} all-reduce(f32[16]{0:T(128)S(1)} %get-tuple-element.8), channel_id=1, replica_groups=mesh['row'=4,'col'=8] {'row','col'}, use_global_device_ids=true, to_apply=%region_14.16 | all-reduce | flops 16 | bytes 128 | tf_op jit(solution)/shard_map/psum | solution.py:14
  385.3 21.4 %reduce-scatter.14.cloned.1.call-done = f32[2,16,256]{2,1,0:T(8,128)} async-done(((f32[16,16,256]{2,1,0:T(8,128)}), f32[2,16,256]{2,1,0:T(8,128)}) %reduce-scatter.14.cloned.1.call-update) | async-done | bytes 32784 | tf_op jit(solution)/shard_map/reduce_scatter | solution.py:43
  406.7 1.4 broadcast_divide_fusion
  (12 shorter events, 0.1 us)
Async XLA Ops:
  6.5 84.6 %reduce-scatter.6.cloned.1.call-start = ((), (), s32[]{:S(2)}) async-start(), calls=%async_computation.5 | async-start | bytes 294912 | tf_op jit(solution)/shard_map/reduce_scatter | solution.py:43
  26.7 143.2 %reduce-scatter.8.cloned.1.call-start = ((), (), s32[]{:S(2)}) async-start(), calls=%async_computation.6 | async-start | bytes 294912 | tf_op jit(solution)/shard_map/reduce_scatter | solution.py:43
  108.3 140.6 %reduce-scatter.10.cloned.1.call-start = ((), (), s32[]{:S(2)}) async-start(), calls=%async_computation.7 | async-start | bytes 294912 | tf_op jit(solution)/shard_map/reduce_scatter | solution.py:43
  187.3 140.4 %reduce-scatter.12.cloned.1.call-start = ((), (), s32[]{:S(2)}) async-start(), calls=%async_computation.8 | async-start | bytes 294912 | tf_op jit(solution)/shard_map/reduce_scatter | solution.py:43
  266.1 140.6 %reduce-scatter.14.cloned.1.call-start = ((), (), s32[]{:S(2)}) async-start(), calls=%async_computation.9 | async-start | bytes 294912 | tf_op jit(solution)/shard_map/reduce_scatter | solution.py:43
Sparse Core Ops, SparseCore 0:
  26.8 64.2 reduce-scatter.5
  108.4 61.4 reduce-scatter.7
  187.4 61.4 reduce-scatter.9
  266.2 61.4 reduce-scatter.11
  345.2 61.4 reduce-scatter.13
where the time goes:
time: 416 us; the launch traced here: 415 us
  blocking collectives  229 us (55%)
  waiting for transfers between devices  109 us (26%)
  matrix products  47.3 us (11%)
  between operations  13.9 us (3%)
  local copies, waits for them, and re-layouts  8.01 us (2%)
  other arithmetic  6.91 us (2%)
    psum x5, blocking collectives, column_rms(): squares = lax.psum(local_squares, ('row', 'col'))  202 us
    reduce_scatter x5, waiting for transfers between devices, shards(): lax.psum_scatter(term.reshape(own_blocks * lax.axis_size('col'), vector_c...  109 us
    dot_general x5, matrix products, shards(): jnp.einsum('tkb,tab->tka', picked, stored, preferred_element_type=jnp.flo...  39.8 us
    all_gather x5, blocking collectives, shards(): column_set = lax.all_gather(rounded, 'row', axis=0, tiled=True)  27.5 us
  transfers between devices with their start and end apart: 5, of which 5 were waited for; matrix products, arithmetic and copies ran while one was open for 0% of the time, Pallas kernels for 0%

commit v1 on v0

v1 whole, which is shorter than its diff:
```python
import functools

import jax
import jax.numpy as jnp
from jax import lax
from jax.experimental import pallas as pl
from jax.experimental.pallas import tpu as pltpu
from jax.sharding import PartitionSpec as P

ITERS = 5
epsilon = 1e-06
MESH = pl.DeviceIdType.MESH
BF16 = jnp.bfloat16
F32 = jnp.float32


def largest_divisor(number, limit):
    return max(d for d in range(1, limit + 1) if number % d == 0)


def kernel(
    n_row, n_col, positions, chunk, dense,
    tiles_hbm, cols_ref, table_ref, start_ref, out_ref,
    tiles, flipped, prods, eye, held, v_all, send, rs, own, s_out, s_all,
    tile_sem, ag_send, ag_recv, s_send, s_recv, p_send, p_recv,
):
    capacity, size, _ = tiles.shape
    blocks, vectors, _ = start_ref.shape
    local_cols = n_row * blocks
    r = lax.axis_index("row")
    c = lax.axis_index("col")

    def load(g):
        span = pl.ds(g * chunk, chunk)
        return pltpu.make_async_copy(tiles_hbm.at[0, 0, span], tiles.at[span], tile_sem.at[g])

    for g in range(capacity // chunk):
        load(g).start()

    barrier = pltpu.get_barrier_semaphore()
    for d in range(1, n_row):
        pl.semaphore_signal(barrier, inc=1, device_id={"row": lax.rem(r + d, n_row)}, device_id_type=MESH)
    for d in range(1, n_col):
        pl.semaphore_signal(barrier, inc=1, device_id={"col": lax.rem(c + d, n_col)}, device_id_type=MESH)

    eye[...] = (
        lax.broadcasted_iota(jnp.int32, (size, size), 0) == lax.broadcasted_iota(jnp.int32, (size, size), 1)
    ).astype(F32).astype(BF16)
    prods[capacity] = jnp.zeros((vectors, size), F32)
    flipped[capacity] = jnp.zeros((size, size), BF16)
    diagonal = (
        lax.broadcasted_iota(jnp.int32, (vectors, 128), 0) == lax.broadcasted_iota(jnp.int32, (vectors, 128), 1)
    ).astype(F32)
    pl.semaphore_wait(barrier, n_row + n_col - 2)

    def gather_copy(par, d, source):
        return pltpu.make_async_remote_copy(
            src_ref=v_all.at[par, pl.ds(r * blocks, blocks)],
            dst_ref=v_all.at[par, pl.ds(source * blocks, blocks)],
            send_sem=ag_send.at[d],
            recv_sem=ag_recv.at[par, source],
            device_id={"row": lax.rem(r + d, n_row)},
            device_id_type=MESH,
        )

    def square_copy(par, d, source):
        return pltpu.make_async_remote_copy(
            src_ref=s_out,
            dst_ref=s_all.at[par, source],
            send_sem=s_send.at[d],
            recv_sem=s_recv.at[par, source],
            device_id={"col": lax.rem(c + d, n_col)},
            device_id_type=MESH,
        )

    def part_copy(par, d, source):
        return pltpu.make_async_remote_copy(
            src_ref=send.at[d],
            dst_ref=rs.at[par, source],
            send_sem=p_send.at[d],
            recv_sem=p_recv.at[par, source],
            device_id={"col": lax.rem(c + d, n_col)},
            device_id_type=MESH,
        )

    def share(par, current):
        v_all[par, pl.ds(r * blocks, blocks)] = current.astype(BF16)
        for d in range(1, n_row):
            gather_copy(par, d, r).start()
        for d in range(1, n_row):
            gather_copy(par, d, lax.rem(r + d, n_row)).wait_recv()
        held[...] = v_all[par]
        wide = held[...].astype(F32)
        squares = jnp.sum(wide * wide, axis=0)
        column = jnp.sum(squares, axis=1, keepdims=True)
        row = jnp.sum(column * diagonal, axis=0, keepdims=True)
        s_out[...] = row
        s_all[par, c] = row
        for d in range(1, n_col):
            square_copy(par, d, c).start()

    def looked_up(target, p, j):
        return table_ref[(target * blocks + p) * local_cols + j]

    def sum_products(target, p):
        total = prods[looked_up(target, p, 0)]
        for j in range(1, local_cols):
            total = total + prods[looked_up(target, p, j)]
        return total

    def exchange(par, row_sum, unrolled):
        def one(d):
            target = lax.rem(c + d, n_col)
            for p in range(blocks):
                send[d, p] = row_sum(target, p).astype(BF16)
            part_copy(par, d, c).start()

        if unrolled:
            for d in range(n_col - 1, 0, -1):
                one(d)
        else:
            @pl.loop(1, n_col)
            def _(d):
                one(d)

        for p in range(blocks):
            own[p] = row_sum(c, p)

    def finish(par):
        for d in range(1, n_col):
            square_copy(par, d, lax.rem(c + d, n_col)).wait_recv()
        squares = jnp.sum(s_all[par], axis=0)
        column = jnp.sum(squares * diagonal, axis=1, keepdims=True)
        rms = jnp.sqrt(column / positions + epsilon)
        total = own[...]
        for d in range(1, n_col):
            source = lax.rem(c + d, n_col)
            part_copy(par, d, source).wait_recv()
            total = total + rs[par, source].astype(F32)
        for d in range(1, n_row):
            gather_copy(par, d, r).wait_send()
        for d in range(1, n_col):
            square_copy(par, d, c).wait_send()
            part_copy(par, d, c).wait_send()
        out_ref[...] = total / rms[None]

    share(0, start_ref[...])

    @pl.loop(0, capacity // chunk)
    def _(g):
        load(g).wait()
        for u in range(chunk):
            t = g * chunk + u
            rows = jnp.concatenate([held[cols_ref[t]], eye[...]], axis=0)
            both = lax.dot_general(rows, tiles[t], (((1,), (1,)), ((), ())), preferred_element_type=F32)
            prods[t] = both[:vectors]
            flipped[t] = both[vectors:].astype(BF16)

    exchange(0, sum_products, n_col <= 8)
    finish(0)

    @pl.loop(1, ITERS)
    def _(step):
        par = lax.rem(step, 2)
        share(par, out_ref[...])
        if dense:
            def row_product(target, p):
                total = None
                for j in range(local_cols):
                    term = jnp.dot(held[j], flipped[looked_up(target, p, j)], preferred_element_type=F32)
                    total = term if total is None else total + term
                return total

            exchange(par, row_product, True)
        else:
            @pl.loop(0, capacity // chunk)
            def _(g):
                for u in range(chunk):
                    t = g * chunk + u
                    prods[t] = jnp.dot(held[cols_ref[t]], flipped[t], preferred_element_type=F32)

            exchange(par, sum_products, n_col <= 8)
        finish(par)


def shards(tile_values, tile_index, tile_count, start_vectors):
    n_row, n_col = lax.axis_size("row"), lax.axis_size("col")
    capacity, size = tile_values.shape[2], tile_values.shape[3]
    blocks, vectors, _ = start_vectors.shape
    rows_here, cols_here = n_col * blocks, n_row * blocks
    positions = n_row * n_col * blocks * size
    pairs = rows_here * cols_here
    layout = tile_index[0, 0]
    slots = jnp.arange(capacity, dtype=jnp.int32)
    cells = layout[:, 0] * cols_here + layout[:, 1]
    hit = (jnp.arange(pairs, dtype=jnp.int32)[:, None] == cells[None, :]) & (slots < tile_count[0, 0])[None, :]
    table = capacity + jnp.sum(jnp.where(hit, slots[None, :] - capacity, 0), axis=1)
    chunk = largest_divisor(capacity, 8)
    dense = pairs <= 2 * capacity
    vmem = pl.BlockSpec(memory_space=pltpu.VMEM)
    smem = pl.BlockSpec(memory_space=pltpu.SMEM)
    dma = pltpu.SemaphoreType.DMA
    return pl.pallas_call(
        functools.partial(kernel, n_row, n_col, positions, chunk, dense),
        out_shape=jax.ShapeDtypeStruct(start_vectors.shape, F32),
        in_specs=[pl.BlockSpec(memory_space=pl.ANY), smem, smem, vmem],
        out_specs=vmem,
        scratch_shapes=[
            pltpu.VMEM((capacity, size, size), BF16),
            pltpu.VMEM((capacity + 1, size, size), BF16),
            pltpu.VMEM((capacity + 1, vectors, size), F32),
            pltpu.VMEM((size, size), BF16),
            pltpu.VMEM((cols_here, vectors, size), BF16),
            pltpu.VMEM((2, cols_here, vectors, size), BF16),
            pltpu.VMEM((n_col, blocks, vectors, size), BF16),
            pltpu.VMEM((2, n_col, blocks, vectors, size), BF16),
            pltpu.VMEM((blocks, vectors, size), F32),
            pltpu.VMEM((1, 128), F32),
            pltpu.VMEM((2, n_col, 1, 128), F32),
            dma((capacity // chunk,)),
            dma((n_row,)),
            dma((2, n_row)),
            dma((n_col,)),
            dma((2, n_col)),
            dma((n_col,)),
            dma((2, n_col)),
        ],
        compiler_params=pltpu.CompilerParams(
            collective_id=0, has_side_effects=True, vmem_limit_bytes=48 * 1024 * 1024
        ),
    )(tile_values, layout[:, 1], table, start_vectors)


def solution(mesh):
    return jax.shard_map(
        shards,
        mesh=mesh,
        in_specs=(
            P("row", "col", None, None, None),
            P("row", "col", None, None),
            P("row", "col"),
            P(("row", "col"), None, None),
        ),
        out_specs=P(("row", "col"), None, None),
        check_vma=False,
    )
```

time: 416 us -> 61.6 us (0.15)
  blocking collectives: 229 us -> 0 us
  waiting for transfers between devices: 109 us -> 0 us
  Pallas kernels: 0 us -> 57.7 us
  matrix products: 47.3 us -> 0 us
  between operations: 13.9 us -> 0.68 us
  other arithmetic: 6.91 us -> 0.89 us
  local copies, waits for them, and re-layouts: 8.01 us -> 2.05 us
    psum x5 -> x0, blocking collectives: 202 us -> none  [column_rms(): squares = lax.psum(local_squares, ('row', 'col'))]
    reduce_scatter x5 -> x0, waiting for transfers between devices: 109 us -> none  [shards(): lax.psum_scatter(term.reshape(own_blocks * lax.axis_size('col'), vector_c...]
    pallas_call x0 -> x1, Pallas kernels: none -> 57.7 us  [shards(): pl.pallas_call(functools.partial(kernel, n_row, n_col, positions, chunk,...]
    dot_general x10 -> x0, matrix products: 47.3 us -> none  [the longest x5 39.8 us: shards(): jnp.einsum('tkb,tab->tka', picked, stored, preferred_element_type=jnp.flo...]
    all_gather x5 -> x0, blocking collectives: 27.5 us -> none  [shards(): column_set = lax.all_gather(rounded, 'row', axis=0, tiled=True)]
    reduce_sum x5 -> x1, other arithmetic: 4.73 us -> 0.12 us  [shards(): jnp.sum(jnp.where(hit, slots[None, :] - capacity, 0), axis=1)]
    dot_general x5 -> x0, local copies, waits for them, and re-layouts: 4.24 us -> none  [shards(): term = jnp.dot(onehot, flat_products, precision=lax.Precision.HIGHEST)]
  transfers between devices with their start and end apart: 5 -> 0, of which waited for: 5 -> 0; matrix products, arithmetic and copies ran while one was open for 0% -> 0% of each run, Pallas kernels for 0% -> 0%
where the time goes in v1:
time: 61.6 us; the launch traced here: 61.4 us
  Pallas kernels  57.7 us (94%)
  local copies, waits for them, and re-layouts  2.05 us (3%)
  other arithmetic  0.89 us (1%)
  between operations  0.68 us (1%)
    pallas_call x1, Pallas kernels, shards(): pl.pallas_call(functools.partial(kernel, n_row, n_col, positions, chunk,...  57.7 us
    unnamed x3, local copies, waits for them, and re-layouts  1.37 us

profile of v1, /device:TPU:0, one launch (start us, length us, event | category | flops | bytes accessed | tf_op | source)
XLA Modules:
  0.0 61.4 jit_solution(7517288983576411923)
XLA Ops:
  0.7 0.7 %slice_bitcast_fusion.cols_ref = s32[96]{0:T(128)S(1)} fusion(s32[96,2]{0,1:T(2,128)} %bitcast.9), kind=kLoop, calls=%fused_computation.6 | loop fusion | bytes 768 | tf_op jit(solution)/shard_map/squeeze | solution.py:231
  1.3 0.8 %bitcast_add_fusion = (s32[96]{0:T(128)S(1)}, s32[96]{0:T(128)S(1)}) fusion(s32[96,2]{0,1:T(2,128)} %bitcast.10), kind=kLoop, calls=%fused_computation.3 | loop fusion | flops 288 | bytes 1536 | tf_op jit(solution)/shard_map/add | solution.py:195
  2.1 0.1 select_reduce_fusion
  2.2 0.0 copy-start
  2.2 0.7 %copy-done = f32[2,16,256]{2,1,0:T(8,128)S(1)} copy-done((f32[2,16,256]{2,1,0:T(8,128)S(1)}, f32[2,16,256]{2,1,0:T(8,128)}, u32[]{:S(2)}) %copy-start) | copy-done | bytes 32792
  3.0 57.7 %shard_map.46 = f32[2,16,256]{2,1,0:T(8,128)S(1)} custom-call(bf16[1,1,96,256,256]{4,3,2,1,0:T(8,128)(2,1)} %tiles_hbm.1, s32[96]{0:T(128)S(1)} %slice_bitcast_fusion.cols_ref, s32[128]{0:T(128)S(1)} %broadcast_add_fusion.table_ref, f32[2,16,256]{2,1,0:T(8,128)S(1)} %copy-done), custom_call_target="tpu_custom_call" | custom-call | tf_op jit(solution)/shard_map/pallas_call | solution.py:203
  60.7 0.6 %copy.7 = f32[2,16,256]{2,1,0:T(8,128)} copy(f32[2,16,256]{2,1,0:T(8,128)S(1)} %shard_map.46) | data formatting | bytes 65536
  (2 shorter events, 0.0 us)
Async XLA Ops:
  2.2 0.8 %copy-start = (f32[2,16,256]{2,1,0:T(8,128)S(1)}, f32[2,16,256]{2,1,0:T(8,128)}, u32[]{:S(2)}) copy-start(f32[2,16,256]{2,1,0:T(8,128)} %start_ref.1) | copy-start | bytes 98308

commit v2 on v1

v2 whole, which is shorter than its diff:
```python
import functools

import jax
import jax.numpy as jnp
from jax import lax
from jax.experimental import pallas as pl
from jax.experimental.pallas import tpu as pltpu
from jax.sharding import PartitionSpec as P

ITERS = 5
epsilon = 1e-06
CHUNK = 12
EARLY = 1
READY = 2
MESH = pl.DeviceIdType.MESH
BF16 = jnp.bfloat16
F32 = jnp.float32


def largest_divisor(number, limit):
    return max(d for d in range(1, limit + 1) if number % d == 0)


def row_order(r, n_row):
    partner = r + 1 - 2 * lax.rem(r, 2) if n_row % 2 == 0 else lax.rem(r + 1, n_row)
    base = r - lax.rem(r, 2) if n_row % 2 == 0 else r
    first = [r, partner]
    return first + [lax.rem(base + d, n_row) for d in range(2, n_row)]


def col_peer(c, d, n_col):
    if n_col & (n_col - 1):
        return lax.rem(c + d, n_col)
    peer, bit = 0, 1
    while bit < n_col:
        digit = lax.rem(c // bit, 2)
        peer = peer + bit * (1 - digit if d & bit else digit)
        bit *= 2
    return peer


def kernel(
    n_row, n_col, positions, chunk, early, dense,
    tiles_hbm, index_hbm, count_hbm, start_hbm, out_ref,
    tiles, flipped, prods, eye, held, v_all, send, rs, own, s_out, s_all,
    index_v, cols_ref, count_ref, start_v, table_v, table_ref,
    tile_sem, small_sem, ag_send, ag_recv, s_send, s_recv, p_send, p_recv,
):
    capacity, size, _ = tiles.shape
    blocks, vectors, _ = out_ref.shape
    local_cols = n_row * blocks
    r = lax.axis_index("row")
    c = lax.axis_index("col")

    start_copy = pltpu.make_async_copy(start_hbm, start_v, small_sem.at[0])
    index_copy = pltpu.make_async_copy(index_hbm, index_v, small_sem.at[1])
    count_copy = pltpu.make_async_copy(count_hbm, count_ref, small_sem.at[2])
    cols_copy = pltpu.make_async_copy(index_hbm, cols_ref, small_sem.at[3])
    start_copy.start()
    index_copy.start()
    count_copy.start()
    cols_copy.start()

    def load(g):
        span = pl.ds(g * chunk, chunk)
        return pltpu.make_async_copy(tiles_hbm.at[0, 0, span], tiles.at[span], tile_sem.at[g])

    for g in range(capacity // chunk):
        load(g).start()

    barrier = pltpu.get_barrier_semaphore()
    for d in range(1, n_row):
        pl.semaphore_signal(barrier, inc=1, device_id={"row": lax.rem(r + d, n_row)}, device_id_type=MESH)
    for d in range(1, n_col):
        pl.semaphore_signal(barrier, inc=1, device_id={"col": col_peer(c, d, n_col)}, device_id_type=MESH)

    eye[...] = (
        lax.broadcasted_iota(jnp.int32, (size, size), 0) == lax.broadcasted_iota(jnp.int32, (size, size), 1)
    ).astype(F32).astype(BF16)
    if not dense:
        prods[capacity] = jnp.zeros((vectors, size), F32)
    flipped[capacity] = jnp.zeros((size, size), BF16)
    diagonal = (
        lax.broadcasted_iota(jnp.int32, (vectors, 128), 0) == lax.broadcasted_iota(jnp.int32, (vectors, 128), 1)
    ).astype(F32)

    def flip(low, high):
        @pl.loop(low, high)
        def _(g):
            load(g).wait()
            for u in range(chunk):
                t = g * chunk + u
                if u % 3 == 2:
                    flipped[t] = tiles[t].T
                else:
                    flipped[t] = lax.dot_general(
                        eye[...], tiles[t], (((1,), (1,)), ((), ())), preferred_element_type=F32
                    ).astype(BF16)

    def gather_copy(par, d, source):
        return pltpu.make_async_remote_copy(
            src_ref=v_all.at[par, pl.ds(r * blocks, blocks)],
            dst_ref=v_all.at[par, pl.ds(source * blocks, blocks)],
            send_sem=ag_send.at[d],
            recv_sem=ag_recv.at[par, source],
            device_id={"row": row_order(r, n_row)[d]},
            device_id_type=MESH,
        )

    def square_copy(par, d, source):
        return pltpu.make_async_remote_copy(
            src_ref=s_out,
            dst_ref=s_all.at[par, source],
            send_sem=s_send.at[d],
            recv_sem=s_recv.at[par, source],
            device_id={"col": col_peer(c, d, n_col)},
            device_id_type=MESH,
        )

    def part_copy(par, d, source):
        return pltpu.make_async_remote_copy(
            src_ref=send.at[d],
            dst_ref=rs.at[par, source],
            send_sem=p_send.at[d],
            recv_sem=p_recv.at[par, source],
            device_id={"col": col_peer(c, d, n_col)},
            device_id_type=MESH,
        )

    def share(par, current):
        v_all[par, pl.ds(r * blocks, blocks)] = current.astype(BF16)
        for d in range(1, n_row):
            gather_copy(par, d, r).start()

    def arrive(par, n):
        gather_copy(par, n, row_order(r, n_row)[n]).wait_recv()

    def total_squares(par):
        held[...] = v_all[par]
        wide = held[...].astype(F32)
        squares = jnp.sum(wide * wide, axis=0)
        column = jnp.sum(squares, axis=1, keepdims=True)
        row = jnp.sum(column * diagonal, axis=0, keepdims=True)
        s_out[...] = row
        s_all[par, c] = row
        for d in range(1, n_col):
            square_copy(par, d, c).start()

    def looked_up(target, p, j):
        cell = (target * blocks + p) * local_cols + j
        return table_ref[cell // 128, cell % 128]

    def sum_products(target, p):
        total = prods[looked_up(target, p, 0)]
        for j in range(1, local_cols):
            total = total + prods[looked_up(target, p, j)]
        return total

    def exchange(par, row_sum, unrolled):
        def one(d):
            target = col_peer(c, d, n_col)
            for p in range(blocks):
                send[d, p] = row_sum(target, p).astype(BF16)
            part_copy(par, d, c).start()

        if unrolled:
            for d in range(n_col - 1, 0, -1):
                one(d)
        else:
            for d in range(n_col - 1, 0, -1):
                one(d)

        for p in range(blocks):
            own[p] = row_sum(c, p)

    def finish(par):
        for d in range(1, n_col):
            square_copy(par, d, col_peer(c, d, n_col)).wait_recv()
        squares = jnp.sum(s_all[par], axis=0)
        column = jnp.sum(squares * diagonal, axis=1, keepdims=True)
        rms = jnp.sqrt(column / positions + epsilon)
        total = own[...]
        for d in range(1, n_col):
            source = col_peer(c, d, n_col)
            part_copy(par, d, source).wait_recv()
            total = total + rs[par, source].astype(F32)
        for d in range(1, n_row):
            gather_copy(par, d, r).wait_send()
        for d in range(1, n_col):
            square_copy(par, d, c).wait_send()
            part_copy(par, d, c).wait_send()
        out_ref[...] = total / rms[None]

    start_copy.wait()
    index_copy.wait()
    count_copy.wait()
    cols_copy.wait()
    slots = lax.broadcasted_iota(jnp.int32, (1, capacity), 1)
    cells = index_v[0:1, :] * local_cols + index_v[1:2, :]
    cells = jnp.where(slots < count_ref[0, 0], cells, -1)
    pair = lax.broadcasted_iota(jnp.int32, (128, 1), 0)
    on_diagonal = lax.broadcasted_iota(jnp.int32, (128, 128), 0) == lax.broadcasted_iota(jnp.int32, (128, 128), 1)
    for q in range(table_v.shape[0]):
        found = jnp.sum(jnp.where(pair + q * 128 == cells, slots - capacity, 0), axis=1, keepdims=True)
        table_v[q : q + 1, :] = capacity + jnp.sum(jnp.where(on_diagonal, found, 0), axis=0, keepdims=True)
    table_copy = pltpu.make_async_copy(table_v, table_ref, small_sem.at[4])
    table_copy.start()

    flip(0, early)
    pl.semaphore_wait(barrier, n_row + n_col - 2)
    share(0, start_v[...])
    flip(early, capacity // chunk)
    table_copy.wait()

    @pl.loop(0, ITERS)
    def _(step):
        par = lax.rem(step, 2)
        if dense:
            def add(total, source, target, p):
                for j in range(blocks):
                    term = jnp.dot(
                        v_all[par, source * blocks + j],
                        flipped[looked_up(target, p, source * blocks + j)],
                        preferred_element_type=F32,
                    )
                    total = term if total is None else total + term
                return total

            sources = row_order(r, n_row)
            for n, source in enumerate(sources[:-READY]):
                if n:
                    arrive(par, n)
                for i in range(n_col):
                    for p in range(blocks):
                        prods[i * blocks + p] = add(prods[i * blocks + p] if n else None, source, i, p)
            for n in range(n_row - READY, n_row):
                arrive(par, n)
            total_squares(par)

            def row_product(target, p):
                total = prods[target * blocks + p]
                for source in sources[-READY:]:
                    total = add(total, source, target, p)
                return total

            exchange(par, row_product, True)
        else:
            for n in range(1, n_row):
                arrive(par, n)
            total_squares(par)

            @pl.loop(0, capacity // chunk)
            def _(g):
                for u in range(chunk):
                    t = g * chunk + u
                    prods[t] = jnp.dot(held[cols_ref[1, t]], flipped[t], preferred_element_type=F32)

            exchange(par, sum_products, n_col <= 8)
        finish(par)

        @pl.when(step < ITERS - 1)
        def _():
            share(1 - par, out_ref[...])


def shards(tile_values, tile_index, tile_count, start_vectors):
    n_row, n_col = lax.axis_size("row"), lax.axis_size("col")
    capacity, size = tile_values.shape[2], tile_values.shape[3]
    blocks, vectors, _ = start_vectors.shape
    rows_here, cols_here = n_col * blocks, n_row * blocks
    positions = n_row * n_col * blocks * size
    pairs = rows_here * cols_here
    chunk = largest_divisor(capacity, CHUNK)
    early = min(EARLY, capacity // chunk)
    dense = pairs <= 2 * capacity
    vmem = pl.BlockSpec(memory_space=pltpu.VMEM)
    dma = pltpu.SemaphoreType.DMA
    return pl.pallas_call(
        functools.partial(kernel, n_row, n_col, positions, chunk, early, dense),
        out_shape=jax.ShapeDtypeStruct(start_vectors.shape, F32),
        in_specs=[pl.BlockSpec(memory_space=pltpu.HBM)] * 4,
        out_specs=vmem,
        scratch_shapes=[
            pltpu.VMEM((capacity, size, size), BF16),
            pltpu.VMEM((capacity + 1, size, size), BF16),
            pltpu.VMEM((rows_here if dense else capacity + 1, vectors, size), F32),
            pltpu.VMEM((size, size), BF16),
            pltpu.VMEM((cols_here, vectors, size), BF16),
            pltpu.VMEM((2, cols_here, vectors, size), BF16),
            pltpu.VMEM((n_col, blocks, vectors, size), BF16),
            pltpu.VMEM((2, n_col, blocks, vectors, size), BF16),
            pltpu.VMEM((blocks, vectors, size), F32),
            pltpu.VMEM((1, 128), F32),
            pltpu.VMEM((2, n_col, 1, 128), F32),
            pltpu.VMEM((2, capacity), jnp.int32),
            pltpu.SMEM((2, capacity), jnp.int32),
            pltpu.SMEM((1, 1), jnp.int32),
            pltpu.VMEM(start_vectors.shape, F32),
            pltpu.VMEM((pl.cdiv(pairs, 128), 128), jnp.int32),
            pltpu.SMEM((pl.cdiv(pairs, 128), 128), jnp.int32),
            dma((capacity // chunk,)),
            dma((5,)),
            dma((n_row,)),
            dma((2, n_row)),
            dma((n_col,)),
            dma((2, n_col)),
            dma((n_col,)),
            dma((2, n_col)),
        ],
        compiler_params=pltpu.CompilerParams(
            collective_id=0, has_side_effects=True, vmem_limit_bytes=48 * 1024 * 1024
        ),
    )(tile_values, tile_index[0, 0].T, tile_count, start_vectors)


def solution(mesh):
    return jax.shard_map(
        shards,
        mesh=mesh,
        in_specs=(
            P("row", "col", None, None, None),
            P("row", "col", None, None),
            P("row", "col"),
            P(("row", "col"), None, None),
        ),
        out_specs=P(("row", "col"), None, None),
        check_vma=False,
    )
```

time: 61.6 us -> 51.6 us (0.84)
  Pallas kernels: 57.7 us -> 48.7 us
  other arithmetic: 0.89 us -> 0 us
    pallas_call x1, Pallas kernels: 57.7 us -> 48.7 us  [shards(): pl.pallas_call(functools.partial(kernel, n_row, n_col, positions, chunk,...]
    add x2 -> x0, other arithmetic: 0.76 us -> none  [the longest x1 0.76 us: shards(): cells = layout[:, 0] * cols_here + layout[:, 1]]
    squeeze x1 -> x0, local copies, waits for them, and re-layouts: 0.68 us -> none  [shards(): layout[:, 1]]
    unnamed x3 -> x5, local copies, waits for them, and re-layouts: 1.37 us -> 2.05 us
where the time goes in v2:
time: 51.6 us; the launch traced here: 51.4 us
  Pallas kernels  48.7 us (94%)
  local copies, waits for them, and re-layouts  2.05 us (4%)
  between operations  0.67 us (1%)
    pallas_call x1, Pallas kernels, shards(): pl.pallas_call(functools.partial(kernel, n_row, n_col, positions, chunk,...  48.7 us
    unnamed x5, local copies, waits for them, and re-layouts  2.05 us

profile of v2, /device:TPU:0, one launch (start us, length us, event | category | flops | bytes accessed | tf_op | source)
XLA Modules:
  0.0 51.4 jit_solution(16143232644154083165)
XLA Ops:
  0.7 0.0 copy-start
  0.7 0.7 %copy-done = f32[2,16,256]{2,1,0:T(8,128)S(1)} copy-done((f32[2,16,256]{2,1,0:T(8,128)S(1)}, f32[2,16,256]{2,1,0:T(8,128)}, u32[]{:S(2)}) %copy-start) | copy-done | bytes 32792
  1.4 0.0 copy-start.1
  1.4 0.7 %copy-done.1 = s32[1,1,96,2]{2,3,1,0:T(2,128)S(1)} copy-done((s32[1,1,96,2]{2,3,1,0:T(2,128)S(1)}, s32[1,1,96,2]{2,3,1,0:T(2,128)}, u32[]{:S(2)}) %copy-start.1) | copy-done | bytes 792
  2.1 48.7 %shard_map.46 = f32[2,16,256]{2,1,0:T(8,128)S(1)} custom-call(bf16[1,1,96,256,256]{4,3,2,1,0:T(8,128)(2,1)} %tiles_hbm.1, s32[2,96]{1,0:T(2,128)S(1)} %bitcast.3, s32[1,1]{1,0:T(1,128)S(6)} %copy.6.count_hbm, f32[2,16,256]{2,1,0:T(8,128)S(1)} %copy-done), custom_call_target="tpu_custom_call" | custom-call | tf_op jit(solution)/shard_map/pallas_call | solution.py:278
  50.8 0.6 %copy.7 = f32[2,16,256]{2,1,0:T(8,128)} copy(f32[2,16,256]{2,1,0:T(8,128)S(1)} %shard_map.46) | data formatting | bytes 65536
Async XLA Ops:
  0.7 0.8 %copy-start = (f32[2,16,256]{2,1,0:T(8,128)S(1)}, f32[2,16,256]{2,1,0:T(8,128)}, u32[]{:S(2)}) copy-start(f32[2,16,256]{2,1,0:T(8,128)} %start_hbm.1) | copy-start | bytes 98308
  1.4 0.7 %copy-start.1 = (s32[1,1,96,2]{2,3,1,0:T(2,128)S(1)}, s32[1,1,96,2]{2,3,1,0:T(2,128)}, u32[]{:S(2)}) copy-start(s32[1,1,96,2]{2,3,1,0:T(2,128)} %param.5) | copy-start | bytes 2308
